TPU v7x, 128 devices: a whole 4x4x4 slice. The times are simulated.
128 devices in a mesh: grid: 32 (over x, z, core), orb: 4 (over y).
Axes of the slice: x: 4, y: 4, z: 4, core: 2. Of those that a mesh axis runs over, the one named last changes fastest.
Arguments:
- orbitals: bfloat16 [1800, 262144], P('orb', 'grid'), may hold values from -0.5 to 1.5
- pivots: int32 [3, 96], replicated, may hold values from 0 to 262143, as said below
Outputs:
- cholesky_factor: float32 [262144, 288], P(('grid', 'orb'))
- residual_diagonal: float32 [262144], P(('grid', 'orb'))
- diagonal_peaks: float32 [3], replicated
Inputs may be any that keep to these rules, and one draw needn't show every extreme that they name: `pivots`: all 3 x 96 pivot indices are distinct grid points.
All inputs are finite; a program needn't handle non-finite values.
Results may differ from a plain program's by a relative error of at most 0.0003.
Values may be sent and summed in bfloat16 or wider, within the bound.
No kernel may reach another device: no remote copies, remote signals or barrier semaphores. Data moves between devices by JAX's collectives and lax.ppermute only.
A program may use at most 64 MiB of HBM per device.

v0:
```python
import jax
import jax.numpy as jnp
from jax import lax
from jax.sharding import Mesh
from jax.sharding import PartitionSpec as P

ORB = 1800
GRID = ("grid_0", "grid_1", "grid_2")
GRID_ORB = ("grid_0", "grid_1", "grid_2", "orb")


def from_everyone(x, axis):
    copies = jnp.broadcast_to(x, (lax.axis_size(axis), *x.shape))
    return lax.all_to_all(copies, axis, split_axis=0, concat_axis=0, tiled=True)


def laid_out(pieces, dim):
    pieces = jnp.moveaxis(pieces, 0, dim)
    lengths = pieces.shape
    return pieces.reshape(*lengths[:dim], lengths[dim] * lengths[dim + 1], *lengths[dim + 2 :])


def gather_directly(x, axis, dim):
    pieces = from_everyone(x, axis)
    return laid_out(pieces, dim)


def one_axis_at_a_time(x, axes):
    for axis in axes:
        x = lax.pmax(x, axis)
    return x


def pick_columns(values, index, base, count):
    local = index - base
    inside = (local >= 0) & (local < count)
    taken = jnp.take(values, jnp.clip(local, 0, count - 1), axis=1)
    return jnp.where(inside[None, :], taken, jnp.zeros_like(taken))


def contract_first(left, right):
    return lax.dot_general(
        left, right, (((0,), (0,)), ((), ())), preferred_element_type=jnp.float32
    )


def on_device(orbitals, pivots):
    rows = orbitals.shape[1]
    groups = lax.axis_size("orb")
    share = rows // groups
    sections = pivots.shape[0]
    count = pivots.shape[1]
    total_rank = sections * count
    grid_base = lax.axis_index(GRID) * rows
    squares = lax.psum_scatter(
        jnp.sum(jnp.square(orbitals.astype(jnp.float32)), axis=0),
        "orb",
        scatter_dimension=0,
        tiled=True,
    )
    diagonal = jnp.square(squares / ORB)
    factor = jnp.zeros((share, total_rank), jnp.float32)
    flat = pivots.reshape(total_rank)
    local_pivots = lax.psum(
        pick_columns(orbitals, flat, grid_base, rows).astype(jnp.float32).astype(jnp.bfloat16), GRID
    )
    whole = gather_directly(local_pivots, "orb", 0)
    pivot_pairs = contract_first(whole, whole)
    pivot_factor = jnp.zeros((total_rank, total_rank), jnp.float32)
    peaks = []
    for section in range(sections):
        lead = section * count
        sampled_here = lax.slice_in_dim(local_pivots, lead, lead + count, axis=1)
        known = lax.slice_in_dim(pivot_factor, lead, lead + count, axis=0)
        pair = lax.slice_in_dim(
            lax.slice_in_dim(pivot_pairs, lead, lead + count, axis=0), lead, lead + count, axis=1
        )

        def product(start, length, picked=sampled_here):
            return contract_first(orbitals, picked)

        inner = lax.psum_scatter(
            product(jnp.int32(0), share * lax.axis_size("orb")),
            "orb",
            scatter_dimension=0,
            tiled=True,
        )
        block = jnp.square(pair / ORB) - jnp.dot(known, known.T, precision=lax.Precision.HIGHEST)
        columns = jnp.square(inner / ORB) - jnp.dot(
            factor, known.T, precision=lax.Precision.HIGHEST
        )
        lower = jnp.linalg.cholesky(block)
        fresh = jax.scipy.linalg.solve_triangular(lower, columns.T, lower=True).T
        factor = factor.at[:, lead : lead + count].set(fresh)
        pivot_columns = jnp.square(
            lax.slice_in_dim(pivot_pairs, lead, lead + count, axis=1) / ORB
        ) - jnp.dot(pivot_factor, known.T, precision=lax.Precision.HIGHEST)
        pivot_fresh = jax.scipy.linalg.solve_triangular(lower, pivot_columns.T, lower=True).T
        pivot_factor = pivot_factor.at[:, lead : lead + count].set(pivot_fresh)
        diagonal = diagonal - jnp.sum(fresh * fresh, axis=1)
        peaks.append(one_axis_at_a_time(jnp.max(diagonal), GRID_ORB))
    peak_values = jnp.stack(peaks)
    return (factor, diagonal, peak_values)


def solution(mesh):
    split = Mesh(
        mesh.devices.reshape(4, 4, 2, mesh.shape["orb"]), ("grid_0", "grid_1", "grid_2", "orb")
    )
    placed = (P("orb", GRID), P())
    return jax.shard_map(
        on_device,
        mesh=split,
        in_specs=placed,
        out_specs=(P(GRID_ORB, None), P(GRID_ORB), P()),
        check_vma=False,
    )
```

profile of v0, /device:TPU:0, one launch (start us, length us, event | category | flops | bytes accessed | tf_op | source)
XLA Modules:
  0.0 320.0 jit_solution(15605662126289330419)
XLA Ops:
  7.2 0.7 subtract_clamp_fusion
  7.9 0.1 min.18
  8.0 0.1 min.16
  8.1 0.7 compare_and_fusion.1
  8.8 11.6 %copy.15 = bf16[450,8192]{0,1:T(8,128)(2,1)} copy(bf16[450,8192]{1,0:T(8,128)(2,1)} %param.17) | data formatting | bytes 14745600 | tf_op args[0]
  20.4 0.1 and.39
  20.5 6.5 %gather_fusion = bf16[288,450]{1,0:T(8,128)(2,1)S(1)} fusion(bf16[450,8192]{0,1:T(8,128)(2,1)} %copy.15, s32[1024]{0:T(1024)S(1)} %pad_clamp_fusion), kind=kCustom, calls=%fused_computation | custom fusion | bytes 519552 | tf_op jit(solution)/shard_map/jit(_take)/gather | solution.py:37
  27.0 0.9 select_bitcast_fusion.1
  27.9 0.0 reduce-scatter.4.cloned.1.call-start
  27.9 104.7 %all-reduce.9.cloned.1.call-done = bf16[450,288]{0,1:T(8,128)(2,1)} async-done(((bf16[450,288]{0,1:T(8,128)(2,1)}), bf16[450,288]{0,1:T(8,128)(2,1)}) %all-reduce.9.cloned.1.call-update) | async-done | bytes 259216 | tf_op jit(solution)/shard_map/psum | solution.py:64
  132.7 6.3 %convolution_bitcast_fusion.2 = f32[8192,96]{0,1:T(8,128)} fusion(bf16[450,8192]{1,0:T(8,128)(2,1)} %param.17, bf16[450,288]{0,1:T(8,128)(2,1)} %all-reduce.9.cloned.1.call-done), kind=kOutput, calls=%fused_computation.4 | convolution fusion | flops 707788800 | bytes 10715136 | tf_op jit(solution)/shard_map/dot_general | solution.py:42
  139.0 0.0 reduce-scatter.6.cloned.1.call-start
  139.1 0.9 copy-done.2
  140.0 6.3 %convolution_bitcast_fusion.1 = f32[8192,96]{0,1:T(8,128)} fusion(bf16[450,8192]{1,0:T(8,128)(2,1)} %param.17, bf16[450,288]{0,1:T(8,128)(2,1)S(1)} %copy-done.2), kind=kOutput, calls=%fused_computation.3 | convolution fusion | flops 707788800 | bytes 10616832 | tf_op jit(solution)/shard_map/dot_general | solution.py:42
  146.3 0.0 reduce-scatter.8.cloned.1.call-start
  146.3 6.6 %convolution_bitcast_fusion = f32[8192,96]{0,1:T(8,128)} fusion(bf16[450,8192]{1,0:T(8,128)(2,1)} %param.17, bf16[450,288]{0,1:T(8,128)(2,1)S(1)} %copy-done.2), kind=kOutput, calls=%fused_computation.2 | convolution fusion | flops 707788800 | bytes 10616832 | tf_op jit(solution)/shard_map/dot_general | solution.py:42
  152.9 1.1 broadcast_in_dim.32
  154.1 4.3 %all-to-all-start = ((bf16[4,450,288]{1,2,0:T(8,128)(2,1)}), bf16[4,450,288]{1,2,0:T(8,128)(2,1)S(1)}, u32[]{:S(2)}, u32[]{:S(2)}) async-start(bf16[4,450,288]{1,2,0:T(8,128)(2,1)} %broadcast_in_dim.32), calls=%async_computation | async-start | bytes 2359296 | tf_op jit(solution)/shard_map/all_to_all | solution.py:14
  158.4 0.6 dynamic-slice.43
  159.6 0.6 compare_reduce_fusion.4
  160.3 0.7 compare_reduce_fusion.3
  161.0 4.8 %multiply_reduce_fusion = f32[8192]{0:T(1024)S(1)} fusion(bf16[450,8192]{1,0:T(8,128)(2,1)} %param.17), kind=kLoop, calls=%fused_computation.1 | loop fusion | flops 11051008 | bytes 7405568 | tf_op jit(solution)/shard_map/reduce_sum | solution.py:56
  165.8 31.0 %all-reduce.2 = f32[8192]{0:T(1024)S(1)} all-reduce(f32[8192]{0:T(1024)S(1)} %multiply_reduce_fusion), channel_id=5, replica_groups=mesh['grid_0'=4,'grid_1'=4,'grid_2'=2,'orb'=4] {'orb'}, use_global_device_ids=true, to_apply=%region_9.13.clone | all-reduce | flops 8192 | bytes 65536
  196.8 0.8 convolution_bitcast_fusion.4
  197.6 0.1 fusion.49
  197.7 0.1 copy.28
  197.8 0.3 convolution_subtract_fusion.5
  198.0 0.1 copy.18
  198.1 8.8 %cholesky.59 = f32[96,96]{1,0:T(8,128)S(1)} custom-call(f32[96,96]{1,0:T(8,128)S(1)} %fusion.36), custom_call_target="Cholesky" | custom-call | tf_op jit(solution)/shard_map/jit(cholesky)/cholesky | solution.py:92
  206.9 0.6 compare_reduce_fusion.2
  207.6 0.7 fusion.25
  208.2 7.4 %custom-call.11 = f32[1,96,96]{1,2,0:T(8,128)S(1)} custom-call(f32[1,96,96]{2,1,0:T(8,128)S(1)} %fusion.25), custom_call_target="InvertDiagBlocksLowerTriangular" | custom-call | tf_op jit(solution)/shard_map/jit(_solve_triangular)/triangular_solve | solution.py:93
  215.6 0.1 copy.29
  215.7 1.0 fusion.5
  216.7 0.4 convolution_subtract_fusion.4
  217.1 0.1 copy.21
  217.2 8.8 %cholesky.70 = f32[96,96]{1,0:T(8,128)S(1)} custom-call(f32[96,96]{1,0:T(8,128)S(1)} %fusion.33), custom_call_target="Cholesky" | custom-call | tf_op jit(solution)/shard_map/jit(cholesky)/cholesky | solution.py:92
  226.0 0.6 compare_reduce_fusion.1
  226.7 0.7 fusion.26
  227.4 7.4 %custom-call.13 = f32[1,96,96]{1,2,0:T(8,128)S(1)} custom-call(f32[1,96,96]{2,1,0:T(8,128)S(1)} %fusion.26), custom_call_target="InvertDiagBlocksLowerTriangular" | custom-call | tf_op jit(solution)/shard_map/jit(_solve_triangular)/triangular_solve | solution.py:93
  234.8 0.1 copy.30
  234.8 0.6 fusion.2
  235.4 1.0 fusion.4
  236.4 0.6 convolution_subtract_fusion.3
  237.0 0.1 copy.24
  237.1 8.9 %cholesky.81 = f32[96,96]{1,0:T(8,128)S(1)} custom-call(f32[96,96]{1,0:T(8,128)S(1)} %fusion.29), custom_call_target="Cholesky" | custom-call | tf_op jit(solution)/shard_map/jit(cholesky)/cholesky | solution.py:92
  246.1 0.6 compare_reduce_fusion
  246.7 0.7 fusion.27
  247.4 7.4 %custom-call.15 = f32[1,96,96]{1,2,0:T(8,128)S(1)} custom-call(f32[1,96,96]{2,1,0:T(8,128)S(1)} %fusion.27), custom_call_target="InvertDiagBlocksLowerTriangular" | custom-call | tf_op jit(solution)/shard_map/jit(_solve_triangular)/triangular_solve | solution.py:93
  254.8 2.7 multiply_reduce_fusion.3
  257.5 0.2 scatter.16
  257.7 2.3 fusion.1
  260.1 1.5 bitcast_dynamic-update-slice_fusion
  261.6 0.1 multiply_reduce_fusion.2
  261.6 8.3 %reduce-scatter.8.cloned.1.call-done = f32[2048,96]{0,1:T(8,128)} async-done(((f32[8192,96]{0,1:T(8,128)}), f32[2048,96]{0,1:T(8,128)}) %reduce-scatter.8.cloned.1.call-update) | async-done | bytes 786448 | tf_op jit(solution)/shard_map/reduce_scatter | solution.py:82
  270.0 3.3 %fusion = f32[96,2048]{1,0:T(8,128)S(1)} fusion(f32[2048,288]{0,1:T(8,128)S(1)} %get-tuple-element.90, f32[2048,96]{0,1:T(8,128)} %reduce-scatter.8.cloned.1.call-done, f32[288,288]{0,1:T(8,128)} %copy-done.1), kind=kOutput, calls=%fused_computation.7 | convolution fusion | flops 680067072 | bytes 4079616 | tf_op jit(solution)/shard_map/dot_general | solution.py:89
  273.3 0.9 multiply_reduce_fusion.1
  274.2 0.8 fusion.46
  274.9 1.3 fusion.48
  276.2 11.1 %all-reduce.5 = (f32[]{:T(128)}, f32[]{:T(128)}, f32[]{:T(128)}) all-reduce(f32[]{:T(128)} %get-tuple-element.81, f32[]{:T(128)} %get-tuple-element.67, f32[]{:T(128)} %get-tuple-element.66), channel_id=1, replica_groups=mesh['grid_0'=4,'grid_1'=4,'grid_2'=2,'orb'=4] {'grid_0'}, use_global_device_ids=true, to_apply=%region_24.28 | all-reduce | flops 3 | bytes 24 | tf_op jit(solution)/shard_map/pmax | solution.py:30
  287.3 11.3 %all-reduce.4 = (f32[]{:T(128)}, f32[]{:T(128)}, f32[]{:T(128)}) all-reduce(f32[]{:T(128)} %get-tuple-element.74, f32[]{:T(128)} %get-tuple-element.75, f32[]{:T(128)} %get-tuple-element.76), channel_id=1, replica_groups=mesh['grid_0'=4,'grid_1'=4,'grid_2'=2,'orb'=4] {'grid_1'}, use_global_device_ids=true, to_apply=%region_25.29 | all-reduce | flops 3 | bytes 24 | tf_op jit(solution)/shard_map/pmax | solution.py:30
  298.6 3.2 all-reduce.6
  301.8 9.2 %all-reduce.3 = (f32[1]{0:T(128)}, f32[1]{0:T(128)}, f32[1]{0:T(128)}) all-reduce(f32[1]{0:T(128)} %bitcast.30, f32[1]{0:T(128)} %bitcast.29, f32[1]{0:T(128)} %bitcast.28), channel_id=1, replica_groups=mesh['grid_0'=4,'grid_1'=4,'grid_2'=2,'orb'=4] {'orb'}, use_global_device_ids=true, to_apply=%region_27.31 | all-reduce | flops 3 | bytes 24 | tf_op jit(solution)/shard_map/pmax | solution.py:30
  311.0 2.5 pad_maximum_fusion
  (25 shorter events, 0.4 us)
Async XLA Ops:
  7.2 125.5 %all-reduce.9.cloned.1.call-start = ((), (), s32[]{:S(2)}) async-start(), calls=%async_computation.4 | async-start | bytes 589824 | tf_op jit(solution)/shard_map/psum | solution.py:64
  27.9 226.9 %reduce-scatter.4.cloned.1.call-start = ((), (), s32[]{:S(2)}) async-start(), calls=%async_computation.5 | async-start | bytes 3932160 | tf_op jit(solution)/shard_map/reduce_scatter | solution.py:82
  139.0 1.0 copy-start.2
  139.0 118.7 %reduce-scatter.6.cloned.1.call-start = ((), (), s32[]{:S(2)}) async-start(), calls=%async_computation.6 | async-start | bytes 3932160 | tf_op jit(solution)/shard_map/reduce_scatter | solution.py:82
  146.3 123.7 %reduce-scatter.8.cloned.1.call-start = ((), (), s32[]{:S(2)}) async-start(), calls=%async_computation.7 | async-start | bytes 3932160 | tf_op jit(solution)/shard_map/reduce_scatter | solution.py:82
  152.9 5.5 %copy-start.3 = (u32[128]{0:T(128)S(1)}, u32[128]{0:T(128)}, u32[]{:S(2)}) copy-start(u32[128]{0:T(128)} %constant.233) | copy-start | bytes 1540
  154.1 42.7 %all-to-all-start = ((bf16[4,450,288]{1,2,0:T(8,128)(2,1)}), bf16[4,450,288]{1,2,0:T(8,128)(2,1)S(1)}, u32[]{:S(2)}, u32[]{:S(2)}) async-start(bf16[4,450,288]{1,2,0:T(8,128)(2,1)} %broadcast_in_dim.32), calls=%async_computation | async-start | bytes 2359296 | tf_op jit(solution)/shard_map/all_to_all | solution.py:14
  236.4 21.0 %copy-start.1 = (f32[288,288]{0,1:T(8,128)}, f32[288,288]{0,1:T(8,128)S(1)}, u32[]{:S(2)}) copy-start(f32[288,288]{0,1:T(8,128)S(1)} %fusion.4) | copy-start | bytes 995332
  274.1 39.3 %copy-start = (f32[2048,288]{0,1:T(8,128)}, f32[2048,288]{0,1:T(8,128)S(1)}, u32[]{:S(2)}) copy-start(f32[2048,288]{0,1:T(8,128)S(1)} %get-tuple-element.86) | copy-start | bytes 7077892
Sparse Core Ops, SparseCore 0:
  28.0 104.6 all-reduce.8
  139.1 49.4 reduce-scatter.3
  191.1 38.4 reduce-scatter.5
  231.8 38.0 reduce-scatter.7
where the time goes:
time: 321 us; the launch traced here: 320 us
  waiting for transfers between devices  113 us (35%)
  blocking collectives  65.8 us (20%)
  other arithmetic  65.6 us (20%)
  matrix products  34.5 us (11%)
  local copies, waits for them, and re-layouts  21.8 us (7%)
  between operations  14.8 us (5%)
  starting transfers between devices  4.49 us (1%)
    psum x1, waiting for transfers between devices, on_device(): lax.psum(pick_columns(orbitals, flat, grid_base, rows).astype(jnp.float32...  105 us
    pmax x4, blocking collectives, one_axis_at_a_time(): x = lax.pmax(x, axis)  34.8 us
    unnamed x1, blocking collectives  31 us
    another operation x9, other arithmetic, on_device(): lower = jnp.linalg.cholesky(block)  28.5 us
    another operation x6, other arithmetic, on_device(): fresh = jax.scipy.linalg.solve_triangular(lower, columns.T, lower=True).T  24 us
    dot_general x4, matrix products, contract_first(): lax.dot_general(left, right, (((0,), (0,)), ((), ())), preferred_element_...  20 us
    unnamed x13, local copies, waits for them, and re-layouts  13.3 us
    reduce_scatter x3, waiting for transfers between devices, on_device(): lax.psum_scatter(product(jnp.int32(0), share * lax.axis_size('orb')), 'or...  8.36 us
  transfers between devices with their start and end apart: 5, of which 2 were waited for; matrix products, arithmetic and copies ran while one was open for 27% of the time, Pallas kernels for 0%

commit v1 on v0

--- a/solution.py
+++ b/solution.py
@@ -62,7 +62,11 @@
     factor = jnp.zeros((share, total_rank), jnp.float32)
     flat = pivots.reshape(total_rank)
     local_pivots = lax.psum(
-        pick_columns(orbitals, flat, grid_base, rows).astype(jnp.float32).astype(jnp.bfloat16), GRID
+        lax.psum(
+            pick_columns(orbitals, flat, grid_base, rows).astype(jnp.float32).astype(jnp.bfloat16),
+            ("grid_1", "grid_2"),
+        ),
+        "grid_0",
     )
     whole = gather_directly(local_pivots, "orb", 0)
     pivot_pairs = contract_first(whole, whole)

time: 321 us -> 324 us (level)
    psum x0 -> x1, waiting for transfers between devices: none -> 42.9 us  [on_device(): lax.psum(lax.psum(pick_columns(orbitals, flat, grid_base, rows).astype(jn...]
    psum x1, waiting for transfers between devices: 105 us -> 63.4 us  [on_device(): lax.psum(pick_columns(orbitals, flat, grid_base, rows).astype(jnp.float32...]
  transfers between devices with their start and end apart: 5 -> 6, of which waited for: 2 -> 3; matrix products, arithmetic and copies ran while one was open for 27% -> 26% of each run, Pallas kernels for 0% -> 0%
where the time goes in v1:
time: 324 us; the launch traced here: 323 us
  waiting for transfers between devices  116 us (36%)
  blocking collectives  66 us (20%)
  other arithmetic  65.6 us (20%)
  matrix products  34.8 us (11%)
  local copies, waits for them, and re-layouts  21.8 us (7%)
  between operations  14.8 us (5%)
  starting transfers between devices  4.48 us (1%)
    psum x1, waiting for transfers between devices, on_device(): lax.psum(pick_columns(orbitals, flat, grid_base, rows).astype(jnp.float32...  63.4 us
    psum x1, waiting for transfers between devices, on_device(): lax.psum(lax.psum(pick_columns(orbitals, flat, grid_base, rows).astype(jn...  42.9 us
    pmax x4, blocking collectives, one_axis_at_a_time(): x = lax.pmax(x, axis)  34.9 us
    unnamed x1, blocking collectives  31.2 us
    another operation x9, other arithmetic, on_device(): lower = jnp.linalg.cholesky(block)  28.5 us
    another operation x6, other arithmetic, on_device(): fresh = jax.scipy.linalg.solve_triangular(lower, columns.T, lower=True).T  24 us
    dot_general x4, matrix products, contract_first(): lax.dot_general(left, right, (((0,), (0,)), ((), ())), preferred_element_...  20.4 us
    unnamed x13, local copies, waits for them, and re-layouts  13.3 us
  transfers between devices with their start and end apart: 6, of which 3 were waited for; matrix products, arithmetic and copies ran while one was open for 26% of the time, Pallas kernels for 0%

profile of v1, /device:TPU:0, one launch (start us, length us, event | category | flops | bytes accessed | tf_op | source)
XLA Modules:
  0.0 323.3 jit_solution(10848617563473438924)
XLA Ops:
  7.2 0.7 subtract_clamp_fusion
  7.9 0.1 min.18
  8.0 0.1 min.16
  8.1 0.7 compare_and_fusion.1
  8.8 11.6 %copy.15 = bf16[450,8192]{0,1:T(8,128)(2,1)} copy(bf16[450,8192]{1,0:T(8,128)(2,1)} %param.17) | data formatting | bytes 14745600 | tf_op args[0]
  20.4 0.1 and.39
  20.5 6.5 %gather_fusion = bf16[288,450]{1,0:T(8,128)(2,1)S(1)} fusion(bf16[450,8192]{0,1:T(8,128)(2,1)} %copy.15, s32[1024]{0:T(1024)S(1)} %pad_clamp_fusion), kind=kCustom, calls=%fused_computation | custom fusion | bytes 519552 | tf_op jit(solution)/shard_map/jit(_take)/gather | solution.py:37
  27.0 0.9 select_bitcast_fusion.1
  27.9 0.0 all-reduce.12.cloned.1.call-start
  27.9 63.4 %all-reduce.10.cloned.1.call-done = bf16[450,288]{0,1:T(8,128)(2,1)} async-done(((bf16[450,288]{0,1:T(8,128)(2,1)}), bf16[450,288]{0,1:T(8,128)(2,1)}) %all-reduce.10.cloned.1.call-update) | async-done | bytes 259216 | tf_op jit(solution)/shard_map/psum | solution.py:65
  91.4 42.9 %all-reduce.12.cloned.1.call-done = bf16[450,288]{0,1:T(8,128)(2,1)} async-done(((bf16[450,288]{0,1:T(8,128)(2,1)}), bf16[450,288]{0,1:T(8,128)(2,1)}) %all-reduce.12.cloned.1.call-update) | async-done | bytes 259216 | tf_op jit(solution)/shard_map/psum | solution.py:64
  134.3 6.3 %convolution_bitcast_fusion.2 = f32[8192,96]{0,1:T(8,128)} fusion(bf16[450,8192]{1,0:T(8,128)(2,1)} %param.17, bf16[450,288]{0,1:T(8,128)(2,1)} %all-reduce.12.cloned.1.call-done), kind=kOutput, calls=%fused_computation.4 | convolution fusion | flops 707788800 | bytes 10715136 | tf_op jit(solution)/shard_map/dot_general | solution.py:42
  140.6 0.0 reduce-scatter.6.cloned.1.call-start
  140.7 0.9 copy-done.2
  141.6 6.3 %convolution_bitcast_fusion.1 = f32[8192,96]{0,1:T(8,128)} fusion(bf16[450,8192]{1,0:T(8,128)(2,1)} %param.17, bf16[450,288]{0,1:T(8,128)(2,1)S(1)} %copy-done.2), kind=kOutput, calls=%fused_computation.3 | convolution fusion | flops 707788800 | bytes 10616832 | tf_op jit(solution)/shard_map/dot_general | solution.py:42
  148.0 6.9 %convolution_bitcast_fusion = f32[8192,96]{0,1:T(8,128)} fusion(bf16[450,8192]{1,0:T(8,128)(2,1)} %param.17, bf16[450,288]{0,1:T(8,128)(2,1)S(1)} %copy-done.2), kind=kOutput, calls=%fused_computation.2 | convolution fusion | flops 707788800 | bytes 10616832 | tf_op jit(solution)/shard_map/dot_general | solution.py:42
  154.9 1.1 broadcast_in_dim.32
  156.0 4.3 %all-to-all-start = ((bf16[4,450,288]{1,2,0:T(8,128)(2,1)}), bf16[4,450,288]{1,2,0:T(8,128)(2,1)S(1)}, u32[]{:S(2)}, u32[]{:S(2)}) async-start(bf16[4,450,288]{1,2,0:T(8,128)(2,1)} %broadcast_in_dim.32), calls=%async_computation | async-start | bytes 2359296 | tf_op jit(solution)/shard_map/all_to_all | solution.py:14
  160.3 0.6 dynamic-slice.43
  161.5 0.6 compare_reduce_fusion.4
  162.2 0.7 compare_reduce_fusion.3
  162.9 4.8 %multiply_reduce_fusion = f32[8192]{0:T(1024)S(1)} fusion(bf16[450,8192]{1,0:T(8,128)(2,1)} %param.17), kind=kLoop, calls=%fused_computation.1 | loop fusion | flops 11051008 | bytes 7405568 | tf_op jit(solution)/shard_map/reduce_sum | solution.py:56
  167.7 31.2 %all-reduce.2 = f32[8192]{0:T(1024)S(1)} all-reduce(f32[8192]{0:T(1024)S(1)} %multiply_reduce_fusion), channel_id=5, replica_groups=mesh['grid_0'=4,'grid_1'=4,'grid_2'=2,'orb'=4] {'orb'}, use_global_device_ids=true, to_apply=%region_10.14.clone | all-reduce | flops 8192 | bytes 65536
  198.9 0.8 convolution_bitcast_fusion.4
  199.7 0.1 fusion.49
  199.8 0.1 copy.28
  199.9 0.3 convolution_subtract_fusion.5
  200.1 0.1 copy.18
  200.2 8.8 %cholesky.59 = f32[96,96]{1,0:T(8,128)S(1)} custom-call(f32[96,96]{1,0:T(8,128)S(1)} %fusion.36), custom_call_target="Cholesky" | custom-call | tf_op jit(solution)/shard_map/jit(cholesky)/cholesky | solution.py:96
  209.1 0.6 compare_reduce_fusion.2
  209.7 0.7 fusion.25
  210.4 7.4 %custom-call.11 = f32[1,96,96]{1,2,0:T(8,128)S(1)} custom-call(f32[1,96,96]{2,1,0:T(8,128)S(1)} %fusion.25), custom_call_target="InvertDiagBlocksLowerTriangular" | custom-call | tf_op jit(solution)/shard_map/jit(_solve_triangular)/triangular_solve | solution.py:97
  217.7 0.1 copy.29
  217.8 1.0 fusion.5
  218.8 0.4 convolution_subtract_fusion.4
  219.2 0.1 copy.21
  219.3 8.8 %cholesky.70 = f32[96,96]{1,0:T(8,128)S(1)} custom-call(f32[96,96]{1,0:T(8,128)S(1)} %fusion.33), custom_call_target="Cholesky" | custom-call | tf_op jit(solution)/shard_map/jit(cholesky)/cholesky | solution.py:96
  228.2 0.6 compare_reduce_fusion.1
  228.8 0.7 fusion.26
  229.5 7.4 %custom-call.13 = f32[1,96,96]{1,2,0:T(8,128)S(1)} custom-call(f32[1,96,96]{2,1,0:T(8,128)S(1)} %fusion.26), custom_call_target="InvertDiagBlocksLowerTriangular" | custom-call | tf_op jit(solution)/shard_map/jit(_solve_triangular)/triangular_solve | solution.py:97
  236.9 0.1 copy.30
  237.0 0.6 fusion.2
  237.5 1.0 fusion.4
  238.6 0.6 convolution_subtract_fusion.3
  239.1 0.1 copy.24
  239.2 8.9 %cholesky.81 = f32[96,96]{1,0:T(8,128)S(1)} custom-call(f32[96,96]{1,0:T(8,128)S(1)} %fusion.29), custom_call_target="Cholesky" | custom-call | tf_op jit(solution)/shard_map/jit(cholesky)/cholesky | solution.py:96
  248.2 0.6 compare_reduce_fusion
  248.8 0.7 fusion.27
  249.5 7.4 %custom-call.15 = f32[1,96,96]{1,2,0:T(8,128)S(1)} custom-call(f32[1,96,96]{2,1,0:T(8,128)S(1)} %fusion.27), custom_call_target="InvertDiagBlocksLowerTriangular" | custom-call | tf_op jit(solution)/shard_map/jit(_solve_triangular)/triangular_solve | solution.py:97
  256.9 2.6 multiply_reduce_fusion.3
  259.6 0.2 scatter.16
  259.8 2.3 fusion.1
  262.2 1.5 bitcast_dynamic-update-slice_fusion
  263.6 0.1 multiply_reduce_fusion.2
  263.7 9.5 %reduce-scatter.8.cloned.1.call-done = f32[2048,96]{0,1:T(8,128)} async-done(((f32[8192,96]{0,1:T(8,128)}), f32[2048,96]{0,1:T(8,128)}) %reduce-scatter.8.cloned.1.call-update) | async-done | bytes 786448 | tf_op jit(solution)/shard_map/reduce_scatter | solution.py:86
  273.2 3.3 %fusion = f32[96,2048]{1,0:T(8,128)S(1)} fusion(f32[2048,288]{0,1:T(8,128)S(1)} %get-tuple-element.90, f32[2048,96]{0,1:T(8,128)} %reduce-scatter.8.cloned.1.call-done, f32[288,288]{0,1:T(8,128)} %copy-done.1), kind=kOutput, calls=%fused_computation.7 | convolution fusion | flops 680067072 | bytes 4079616 | tf_op jit(solution)/shard_map/dot_general | solution.py:93
  276.5 0.9 multiply_reduce_fusion.1
  277.4 0.8 fusion.46
  278.2 1.3 fusion.48
  279.5 11.1 %all-reduce.5 = (f32[]{:T(128)}, f32[]{:T(128)}, f32[]{:T(128)}) all-reduce(f32[]{:T(128)} %get-tuple-element.81, f32[]{:T(128)} %get-tuple-element.67, f32[]{:T(128)} %get-tuple-element.66), channel_id=1, replica_groups=mesh['grid_0'=4,'grid_1'=4,'grid_2'=2,'orb'=4] {'grid_0'}, use_global_device_ids=true, to_apply=%region_25.29 | all-reduce | flops 3 | bytes 24 | tf_op jit(solution)/shard_map/pmax | solution.py:30
  290.5 11.4 %all-reduce.4 = (f32[]{:T(128)}, f32[]{:T(128)}, f32[]{:T(128)}) all-reduce(f32[]{:T(128)} %get-tuple-element.74, f32[]{:T(128)} %get-tuple-element.75, f32[]{:T(128)} %get-tuple-element.76), channel_id=1, replica_groups=mesh['grid_0'=4,'grid_1'=4,'grid_2'=2,'orb'=4] {'grid_1'}, use_global_device_ids=true, to_apply=%region_26.30 | all-reduce | flops 3 | bytes 24 | tf_op jit(solution)/shard_map/pmax | solution.py:30
  301.9 3.2 all-reduce.6
  305.0 9.3 %all-reduce.3 = (f32[1]{0:T(128)}, f32[1]{0:T(128)}, f32[1]{0:T(128)}) all-reduce(f32[1]{0:T(128)} %bitcast.30, f32[1]{0:T(128)} %bitcast.29, f32[1]{0:T(128)} %bitcast.28), channel_id=1, replica_groups=mesh['grid_0'=4,'grid_1'=4,'grid_2'=2,'orb'=4] {'orb'}, use_global_device_ids=true, to_apply=%region_28.32 | all-reduce | flops 3 | bytes 24 | tf_op jit(solution)/shard_map/pmax | solution.py:30
  314.3 2.5 pad_maximum_fusion
  (28 shorter events, 0.5 us)
Async XLA Ops:
  7.2 84.1 %all-reduce.10.cloned.1.call-start = ((), (), s32[]{:S(2)}) async-start(), calls=%async_computation.4 | async-start | bytes 589824 | tf_op jit(solution)/shard_map/psum | solution.py:65
  27.9 106.4 %all-reduce.12.cloned.1.call-start = ((), (), s32[]{:S(2)}) async-start(), calls=%async_computation.5 | async-start | bytes 589824 | tf_op jit(solution)/shard_map/psum | solution.py:64
  91.3 165.6 %reduce-scatter.4.cloned.1.call-start = ((), (), s32[]{:S(2)}) async-start(), calls=%async_computation.6 | async-start | bytes 3932160 | tf_op jit(solution)/shard_map/reduce_scatter | solution.py:86
  140.6 1.0 copy-start.2
  140.6 119.2 %reduce-scatter.6.cloned.1.call-start = ((), (), s32[]{:S(2)}) async-start(), calls=%async_computation.7 | async-start | bytes 3932160 | tf_op jit(solution)/shard_map/reduce_scatter | solution.py:86
  147.9 125.3 %reduce-scatter.8.cloned.1.call-start = ((), (), s32[]{:S(2)}) async-start(), calls=%async_computation.8 | async-start | bytes 3932160 | tf_op jit(solution)/shard_map/reduce_scatter | solution.py:86
  154.9 5.4 %copy-start.3 = (u32[128]{0:T(128)S(1)}, u32[128]{0:T(128)}, u32[]{:S(2)}) copy-start(u32[128]{0:T(128)} %constant.233) | copy-start | bytes 1540
  156.0 42.9 %all-to-all-start = ((bf16[4,450,288]{1,2,0:T(8,128)(2,1)}), bf16[4,450,288]{1,2,0:T(8,128)(2,1)S(1)}, u32[]{:S(2)}, u32[]{:S(2)}) async-start(bf16[4,450,288]{1,2,0:T(8,128)(2,1)} %broadcast_in_dim.32), calls=%async_computation | async-start | bytes 2359296 | tf_op jit(solution)/shard_map/all_to_all | solution.py:14
  238.5 21.0 %copy-start.1 = (f32[288,288]{0,1:T(8,128)}, f32[288,288]{0,1:T(8,128)S(1)}, u32[]{:S(2)}) copy-start(f32[288,288]{0,1:T(8,128)S(1)} %fusion.4) | copy-start | bytes 995332
  277.4 39.4 %copy-start = (f32[2048,288]{0,1:T(8,128)}, f32[2048,288]{0,1:T(8,128)S(1)}, u32[]{:S(2)}) copy-start(f32[2048,288]{0,1:T(8,128)S(1)} %get-tuple-element.86) | copy-start | bytes 7077892
Sparse Core Ops, SparseCore 0:
  28.0 63.2 all-reduce.9
  93.6 40.5 all-reduce.11
  140.8 51.7 reduce-scatter.3
  194.8 37.9 reduce-scatter.5
  235.1 38.0 reduce-scatter.7
